TPU v7x, 32 devices: a whole 2x2x4 slice. The times are simulated.
32 devices in a mesh: rows: 8 (over z, y), cols: 4 (over x, core).
Axes of the slice: x: 2, y: 2, z: 4, core: 2. Of those that a mesh axis runs over, the one named last changes fastest.
Arguments:
- tile_values: bfloat16 [8, 4, 320, 128, 128], P('rows', 'cols'), may hold values from -0.0625 to 0.0625
- tile_rows: int32 [8, 4, 320], P('rows', 'cols'), may hold values from 0 to 7
- tile_cols: int32 [8, 4, 320], P('rows', 'cols'), may hold values from 0 to 15
- tile_counts: int32 [8, 4], P('rows', 'cols'), may hold values from 1 to 320, as said below
- sketch: bfloat16 [8192, 160], P(('rows', 'cols')), may hold values from -6 to 6
Outputs:
- basis: float32 [8192, 160], P(('rows', 'cols'))
- factor: float32 [160, 160], replicated
Inputs may be any that keep to these rules, and one draw needn't show every extreme that they name: Only the first tile_counts[r, c] slots of list (r, c) are live; some list has all 320 slots live in every draw. `tile_cols`: the same place may stand in several live slots of a list.
All inputs are finite; a program needn't handle non-finite values.
Results may differ from a plain program's by a relative error of at most 0.0029.
Values may be sent and summed in bfloat16 or wider, within the bound.
A program may use at most 128 MiB of HBM per device.

v0:
```python
import math
import jax
import jax.numpy as jnp
from jax import lax
from jax.sharding import PartitionSpec as P

POWER = 2
RT = 8


def accumulate(block_list, row_list, col_list, live_count, gathered, height):
    slot_total = block_list.shape[0]
    tile_size = block_list.shape[1]
    sketch_width = gathered.shape[1]
    tile_stack = gathered.reshape(-1, tile_size, sketch_width)
    block_size = math.gcd(32, slot_total)

    def one_block(block_index, running):
        first_slot = block_index * block_size
        block_values = lax.dynamic_slice_in_dim(block_list, first_slot, block_size, 0)
        rowids = lax.dynamic_slice_in_dim(row_list, first_slot, block_size, 0)
        colids = lax.dynamic_slice_in_dim(col_list, first_slot, block_size, 0)
        picked = jnp.take(tile_stack, colids, axis=0)
        products = jnp.einsum(
            "sab,sbk->sak", block_values, picked, preferred_element_type=jnp.float32
        )
        live_mask = (first_slot + jnp.arange(block_size, dtype=jnp.int32) < live_count).astype(
            jnp.float32
        )
        return running.at[rowids].add(products * live_mask[:, None, None])

    block_count = (live_count + block_size - 1) // block_size
    initial = jnp.zeros((height, tile_size, sketch_width), jnp.float32)
    running = lax.fori_loop(0, block_count, one_block, initial)
    return running.reshape(height * tile_size, sketch_width)


def shards(tile_values, tile_rows, tile_cols, tile_counts, sketch):
    own_values = tile_values[0, 0]
    own_rows = tile_rows[0, 0]
    own_cols = tile_cols[0, 0]
    own_count = tile_counts[0, 0]
    nodes_total = sketch.shape[0] * lax.axis_size("rows") * lax.axis_size("cols")
    current = sketch
    solved = None
    factor = None
    for power in range(POWER):
        gathered = lax.all_gather(current, "rows", axis=0, tiled=True)
        partial_value = accumulate(own_values, own_rows, own_cols, own_count, gathered, RT)
        whole = lax.psum(partial_value, "cols")
        gram_matrix = lax.psum(jnp.dot(whole.T, whole, precision=lax.Precision.HIGHEST), "rows")
        share_rows = whole.shape[0] // lax.axis_size("cols")
        owned = lax.dynamic_slice_in_dim(whole, lax.axis_index("cols") * share_rows, share_rows, 0)
        gram_matrix = gram_matrix / nodes_total
        factor = jnp.linalg.cholesky(gram_matrix)
        solved = lax.linalg.triangular_solve(
            factor, owned, left_side=False, lower=True, transpose_a=True
        )
        current = solved.astype(jnp.bfloat16)
    return (solved, factor)


def solution(mesh):
    placed = (
        P("rows", "cols", None, None, None),
        P("rows", "cols", None),
        P("rows", "cols", None),
        P("rows", "cols"),
        P(("rows", "cols"), None),
    )
    return jax.shard_map(
        shards,
        mesh=mesh,
        in_specs=placed,
        out_specs=(P(("rows", "cols"), None), P()),
        check_vma=False,
    )
```

profile of v0, /device:TPU:0, one launch (start us, length us, event | category | flops | bytes accessed | tf_op | source)
XLA Modules:
  0.0 597.8 jit_solution(8288383398452547619)
XLA Ops:
  9.3 33.6 %all_gather.6 = bf16[2048,160]{0,1:T(8,128)(2,1)S(1)} all-gather(bf16[256,160]{0,1:T(8,128)(2,1)} %param.18), channel_id=1, replica_groups=mesh['rows'=8,'cols'=4] {'rows'}, dimensions={0}, use_global_device_ids=true | all-gather | bytes 737280 | tf_op jit(solution)/shard_map/all_gather | solution.py:48
  44.2 19.8 %while.23 = (s32[]{:T(128)}, f32[8,128,160]{1,2,0:T(8,128)S(1)}, s32[]{:T(128)}, s32[320]{0:T(512)S(1)}, bf16[320,128,128]{2,1,0:T(8,128)(2,1)}, /*index=5*/s32[...) while((s32[]{:T(128)}, f32[8,128,160]{1,2,0:T(8,128)S(1)}, ...), condition=%wide.region_2.4_spmd, body=%wide.region_0.3_spmd.sunk | while | flops 169739648 | bytes 16258423 | solution.py:34
  45.0 3.3 gather_fusion
  51.1 3.0 scatter_fusion
  54.9 3.3 gather_fusion
  61.0 3.0 scatter_fusion
  65.0 110.6 %all-reduce.8.cloned.1.call-done = f32[1024,160]{0,1:T(8,128)} async-done(((f32[1024,160]{0,1:T(8,128)}), f32[1024,160]{0,1:T(8,128)}) %all-reduce.8.cloned.1.call-update) | async-done | bytes 655376 | tf_op jit(solution)/shard_map/psum | solution.py:50
  178.6 71.0 %all-reduce.10.cloned.1.call-done = f32[160,160]{0,1:T(8,128)} async-done(((f32[160,160]{0,1:T(8,128)}), f32[160,160]{0,1:T(8,128)}) %all-reduce.10.cloned.1.call-update) | async-done | bytes 102416 | tf_op jit(solution)/shard_map/psum | solution.py:51
  251.6 11.7 %cholesky.136 = f32[128,128]{1,0:T(8,128)S(1)} custom-call(f32[128,128]{1,0:T(8,128)S(1)} %cholesky.208), custom_call_target="Cholesky" | custom-call | tf_op jit(solution)/shard_map/jit(cholesky)/cholesky | solution.py:55
  263.4 9.8 %custom-call.13 = f32[1,128,128]{1,2,0:T(8,128)S(1)} custom-call(f32[1,128,128]{2,1,0:T(8,128)S(1)} %get-tuple-element.178), custom_call_target="InvertDiagBlocksLowerTriangular" | custom-call | tf_op jit(solution)/shard_map/jit(cholesky)/cholesky | solution.py:55
  273.5 2.9 cholesky.156
  279.2 19.7 %custom-call.14 = f32[2,128,128]{1,2,0:T(8,128)S(1)} custom-call(f32[2,128,128]{2,1,0:T(8,128)S(1)} %pad_maximum_fusion.1), custom_call_target="InvertDiagBlocksLowerTriangular" | custom-call | tf_op jit(solution)/shard_map/triangular_solve/custom-call.0 | solution.py:56
  301.3 32.0 %all_gather.7 = bf16[2048,160]{0,1:T(8,128)(2,1)S(1)} all-gather(bf16[256,160]{0,1:T(8,128)(2,1)S(1)} %maximum_convert_fusion), channel_id=1, replica_groups=mesh['rows'=8,'cols'=4] {'rows'}, dimensions={0}, use_global_device_ids=true | all-gather | bytes 737280 | tf_op jit(solution)/shard_map/all_gather | solution.py:48
  334.7 19.8 %while.24 = (s32[]{:T(128)}, f32[8,128,160]{1,2,0:T(8,128)S(1)}, s32[]{:T(128)}, s32[320]{0:T(512)S(1)}, bf16[320,128,128]{2,1,0:T(8,128)(2,1)}, /*index=5*/s32[...) while((s32[]{:T(128)}, f32[8,128,160]{1,2,0:T(8,128)S(1)}, ...), condition=%wide.region_11.15_spmd, body=%wide.region_9.14_spmd.sunk | while | flops 169739648 | bytes 16258423 | solution.py:34
  335.4 3.3 gather_fusion.1
  341.6 3.0 scatter_fusion.1
  345.3 3.3 gather_fusion.1
  351.5 3.0 scatter_fusion.1
  355.7 108.8 %all-reduce.12.cloned.1.call-done = f32[1024,160]{0,1:T(8,128)} async-done(((f32[1024,160]{0,1:T(8,128)}), f32[1024,160]{0,1:T(8,128)}) %all-reduce.12.cloned.1.call-update) | async-done | bytes 655376 | tf_op jit(solution)/shard_map/psum | solution.py:50
  467.1 71.1 %all-reduce.14.cloned.1.call-done = f32[160,160]{0,1:T(8,128)} async-done(((f32[160,160]{0,1:T(8,128)}), f32[160,160]{0,1:T(8,128)}) %all-reduce.14.cloned.1.call-update) | async-done | bytes 102416 | tf_op jit(solution)/shard_map/psum | solution.py:51
  540.3 11.7 %cholesky.174 = f32[128,128]{1,0:T(8,128)S(1)} custom-call(f32[128,128]{1,0:T(8,128)S(1)} %cholesky.211), custom_call_target="Cholesky" | custom-call | tf_op jit(solution)/shard_map/jit(cholesky)/cholesky | solution.py:55
  552.0 9.8 %custom-call.15 = f32[1,128,128]{1,2,0:T(8,128)S(1)} custom-call(f32[1,128,128]{2,1,0:T(8,128)S(1)} %get-tuple-element.176), custom_call_target="InvertDiagBlocksLowerTriangular" | custom-call | tf_op jit(solution)/shard_map/jit(cholesky)/cholesky | solution.py:55
  562.2 2.9 cholesky.194
  568.5 19.7 %custom-call.16 = f32[2,128,128]{1,2,0:T(8,128)S(1)} custom-call(f32[2,128,128]{2,1,0:T(8,128)S(1)} %pad_maximum_fusion.2), custom_call_target="InvertDiagBlocksLowerTriangular" | custom-call | tf_op jit(solution)/shard_map/triangular_solve/custom-call.0 | solution.py:56
  (75 shorter events, 40.0 us)
Async XLA Ops:
  7.2 168.5 %all-reduce.8.cloned.1.call-start = ((), (), s32[]{:S(2)}) async-start(), calls=%async_computation | async-start | bytes 1310720 | tf_op jit(solution)/shard_map/psum | solution.py:50
  65.0 184.6 %all-reduce.10.cloned.1.call-start = ((), (), s32[]{:S(2)}) async-start(), calls=%async_computation.1 | async-start | bytes 327680 | tf_op jit(solution)/shard_map/psum | solution.py:51
  178.3 286.1 %all-reduce.12.cloned.1.call-start = ((), (), s32[]{:S(2)}) async-start(), calls=%async_computation.2 | async-start | bytes 1310720 | tf_op jit(solution)/shard_map/psum | solution.py:50
  355.4 182.8 %all-reduce.14.cloned.1.call-start = ((), (), s32[]{:S(2)}) async-start(), calls=%async_computation.3 | async-start | bytes 327680 | tf_op jit(solution)/shard_map/psum | solution.py:51
Sparse Core Ops, SparseCore 0:
  65.1 110.4 all-reduce.7
  179.5 70.0 all-reduce.9
  355.5 108.8 all-reduce.11
  468.2 70.0 all-reduce.13
where the time goes:
time: 600 us; the launch traced here: 598 us
  waiting for transfers between devices  362 us (60%)
  other arithmetic  113 us (19%)
  blocking collectives  65.7 us (11%)
  matrix products  21.9 us (4%)
  local copies, waits for them, and re-layouts  17.8 us (3%)
  between operations  17.3 us (3%)
    psum x2, waiting for transfers between devices, shards(): whole = lax.psum(partial_value, 'cols')  219 us
    psum x2, waiting for transfers between devices, shards(): lax.psum(jnp.dot(whole.T, whole, precision=lax.Precision.HIGHEST), 'rows')  142 us
    all_gather x2, blocking collectives, shards(): gathered = lax.all_gather(current, 'rows', axis=0, tiled=True)  65.7 us
    another operation x14, other arithmetic, shards(): factor = jnp.linalg.cholesky(gram_matrix)  51.6 us
    another operation x11, other arithmetic, shards(): lax.linalg.triangular_solve(factor, owned, left_side=False, lower=True, t...  40.9 us
    gather x4, local copies, waits for them, and re-layouts, one_block(): picked = jnp.take(tile_stack, colids, axis=0)  13 us
  transfers between devices with their start and end apart: 4, of which 4 were waited for; matrix products, arithmetic and copies ran while one was open for 0% of the time, Pallas kernels for 0%

commit v1 on v0

--- a/solution.py
+++ b/solution.py
@@ -48,7 +48,9 @@
         gathered = lax.all_gather(current, "rows", axis=0, tiled=True)
         partial_value = accumulate(own_values, own_rows, own_cols, own_count, gathered, RT)
         whole = lax.psum(partial_value, "cols")
-        gram_matrix = lax.psum(jnp.dot(whole.T, whole, precision=lax.Precision.HIGHEST), "rows")
+        gram_matrix = jnp.sum(
+            lax.all_gather(jnp.dot(whole.T, whole, precision=lax.Precision.HIGHEST), "rows"), axis=0
+        )
         share_rows = whole.shape[0] // lax.axis_size("cols")
         owned = lax.dynamic_slice_in_dim(whole, lax.axis_index("cols") * share_rows, share_rows, 0)
         gram_matrix = gram_matrix / nodes_total

time: 600 us -> 523 us (0.87)
  waiting for transfers between devices: 362 us -> 220 us
  blocking collectives: 65.7 us -> 135 us
    psum x2 -> x0, waiting for transfers between devices: 142 us -> none  [shards(): lax.psum(jnp.dot(whole.T, whole, precision=lax.Precision.HIGHEST), 'rows')]
    all_gather x0 -> x2, blocking collectives: none -> 69.4 us  [shards(): lax.all_gather(jnp.dot(whole.T, whole, precision=lax.Precision.HIGHEST),...]
  transfers between devices with their start and end apart: 4 -> 2, of which waited for: 4 -> 2; matrix products, arithmetic and copies ran while one was open for 0% -> 0% of each run, Pallas kernels for 0% -> 0%
where the time goes in v1:
time: 523 us; the launch traced here: 521 us
  waiting for transfers between devices  220 us (42%)
  blocking collectives  135 us (26%)
  other arithmetic  109 us (21%)
  matrix products  20.6 us (4%)
  local copies, waits for them, and re-layouts  18 us (3%)
  between operations  17.6 us (3%)
    psum x2, waiting for transfers between devices, shards(): whole = lax.psum(partial_value, 'cols')  220 us
    all_gather x2, blocking collectives, shards(): lax.all_gather(jnp.dot(whole.T, whole, precision=lax.Precision.HIGHEST),...  69.4 us
    all_gather x2, blocking collectives, shards(): gathered = lax.all_gather(current, 'rows', axis=0, tiled=True)  65.4 us
    another operation x14, other arithmetic, shards(): factor = jnp.linalg.cholesky(gram_matrix)  51.6 us
    another operation x11, other arithmetic, shards(): lax.linalg.triangular_solve(factor, owned, left_side=False, lower=True, t...  40.9 us
    gather x4, local copies, waits for them, and re-layouts, one_block(): picked = jnp.take(tile_stack, colids, axis=0)  13 us
    scatter-add x4, other arithmetic, one_block(): return running.at[rowids].add(products * live_mask[:, None, None])  11.9 us
    dot_general x4, matrix products, one_block(): jnp.einsum('sab,sbk->sak', block_values, picked, preferred_element_type=j...  11.2 us
  transfers between devices with their start and end apart: 2, of which 2 were waited for; matrix products, arithmetic and copies ran while one was open for 0% of the time, Pallas kernels for 0%

profile of v1, /device:TPU:0, one launch (start us, length us, event | category | flops | bytes accessed | tf_op | source)
XLA Modules:
  0.0 521.0 jit_solution(1084597358462860088)
XLA Ops:
  9.3 33.6 %all_gather.18 = bf16[2048,160]{0,1:T(8,128)(2,1)S(1)} all-gather(bf16[256,160]{0,1:T(8,128)(2,1)} %param.18), channel_id=1, replica_groups=mesh['rows'=8,'cols'=4] {'rows'}, dimensions={0}, use_global_device_ids=true | all-gather | bytes 737280 | tf_op jit(solution)/shard_map/all_gather | solution.py:48
  44.2 19.8 %while.23 = (s32[]{:T(128)}, f32[8,128,160]{1,2,0:T(8,128)S(1)}, s32[]{:T(128)}, s32[320]{0:T(512)S(1)}, bf16[320,128,128]{2,1,0:T(8,128)(2,1)}, /*index=5*/s32[...) while((s32[]{:T(128)}, f32[8,128,160]{1,2,0:T(8,128)S(1)}, ...), condition=%wide.region_2.4_spmd, body=%wide.region_0.3_spmd.sunk | while | flops 169739648 | bytes 16258423 | solution.py:34
  45.0 3.3 gather_fusion
  51.1 3.0 scatter_fusion
  54.9 3.3 gather_fusion
  61.0 3.0 scatter_fusion
  65.1 110.6 %all-reduce.6.cloned.1.call-done = f32[1024,160]{0,1:T(8,128)} async-done(((f32[1024,160]{0,1:T(8,128)}), f32[1024,160]{0,1:T(8,128)}) %all-reduce.6.cloned.1.call-update) | async-done | bytes 655376 | tf_op jit(solution)/shard_map/psum | solution.py:50
  177.6 34.8 %all-gather = f32[1280,160]{1,0:T(8,128)S(1)} all-gather(f32[160,160]{1,0:T(8,128)S(1)} %fusion.45), channel_id=2, replica_groups=mesh['rows'=8,'cols'=4] {'rows'}, dimensions={0}, use_global_device_ids=true | all-gather | bytes 921600 | tf_op jit(solution)/shard_map/all_gather | solution.py:52
  212.8 11.7 %cholesky.136 = f32[128,128]{1,0:T(8,128)S(1)} custom-call(f32[128,128]{1,0:T(8,128)S(1)} %cholesky.208), custom_call_target="Cholesky" | custom-call | tf_op jit(solution)/shard_map/jit(cholesky)/cholesky | solution.py:57
  224.5 9.8 %custom-call.13 = f32[1,128,128]{1,2,0:T(8,128)S(1)} custom-call(f32[1,128,128]{2,1,0:T(8,128)S(1)} %get-tuple-element.186), custom_call_target="InvertDiagBlocksLowerTriangular" | custom-call | tf_op jit(solution)/shard_map/jit(cholesky)/cholesky | solution.py:57
  234.7 2.9 cholesky.156
  240.4 19.7 %custom-call.14 = f32[2,128,128]{1,2,0:T(8,128)S(1)} custom-call(f32[2,128,128]{2,1,0:T(8,128)S(1)} %pad_maximum_fusion.1), custom_call_target="InvertDiagBlocksLowerTriangular" | custom-call | tf_op jit(solution)/shard_map/triangular_solve/custom-call.0 | solution.py:58
  262.5 31.7 %all_gather.21 = bf16[2048,160]{0,1:T(8,128)(2,1)S(1)} all-gather(bf16[256,160]{0,1:T(8,128)(2,1)S(1)} %maximum_convert_fusion), channel_id=1, replica_groups=mesh['rows'=8,'cols'=4] {'rows'}, dimensions={0}, use_global_device_ids=true | all-gather | bytes 737280 | tf_op jit(solution)/shard_map/all_gather | solution.py:48
  295.6 20.0 %while.24 = (s32[]{:T(128)}, f32[8,128,160]{1,2,0:T(8,128)S(1)}, s32[]{:T(128)}, s32[320]{0:T(512)S(1)}, bf16[320,128,128]{2,1,0:T(8,128)(2,1)}, /*index=5*/s32[...) while((s32[]{:T(128)}, f32[8,128,160]{1,2,0:T(8,128)S(1)}, ...), condition=%wide.region_11.15_spmd, body=%wide.region_9.14_spmd.sunk | while | flops 169739648 | bytes 16258423 | solution.py:34
  296.6 3.3 gather_fusion.1
  302.7 3.0 scatter_fusion.1
  306.4 3.3 gather_fusion.1
  312.6 3.0 scatter_fusion.1
  316.5 109.6 %all-reduce.8.cloned.1.call-done = f32[1024,160]{0,1:T(8,128)} async-done(((f32[1024,160]{0,1:T(8,128)}), f32[1024,160]{0,1:T(8,128)}) %all-reduce.8.cloned.1.call-update) | async-done | bytes 655376 | tf_op jit(solution)/shard_map/psum | solution.py:50
  428.1 34.6 %all-gather.1 = f32[1280,160]{1,0:T(8,128)S(1)} all-gather(f32[160,160]{1,0:T(8,128)S(1)} %fusion.46), channel_id=3, replica_groups=mesh['rows'=8,'cols'=4] {'rows'}, dimensions={0}, use_global_device_ids=true | all-gather | bytes 921600 | tf_op jit(solution)/shard_map/all_gather | solution.py:52
  463.1 11.7 %cholesky.174 = f32[128,128]{1,0:T(8,128)S(1)} custom-call(f32[128,128]{1,0:T(8,128)S(1)} %cholesky.211), custom_call_target="Cholesky" | custom-call | tf_op jit(solution)/shard_map/jit(cholesky)/cholesky | solution.py:57
  474.9 9.8 %custom-call.15 = f32[1,128,128]{1,2,0:T(8,128)S(1)} custom-call(f32[1,128,128]{2,1,0:T(8,128)S(1)} %get-tuple-element.184), custom_call_target="InvertDiagBlocksLowerTriangular" | custom-call | tf_op jit(solution)/shard_map/jit(cholesky)/cholesky | solution.py:57
  485.0 2.9 cholesky.194
  491.4 19.7 %custom-call.16 = f32[2,128,128]{1,2,0:T(8,128)S(1)} custom-call(f32[2,128,128]{2,1,0:T(8,128)S(1)} %pad_maximum_fusion.2), custom_call_target="InvertDiagBlocksLowerTriangular" | custom-call | tf_op jit(solution)/shard_map/triangular_solve/custom-call.0 | solution.py:58
  (75 shorter events, 34.9 us)
Async XLA Ops:
  7.2 168.5 %all-reduce.6.cloned.1.call-start = ((), (), s32[]{:S(2)}) async-start(), calls=%async_computation | async-start | bytes 1310720 | tf_op jit(solution)/shard_map/psum | solution.py:50
  65.0 361.2 %all-reduce.8.cloned.1.call-start = ((), (), s32[]{:S(2)}) async-start(), calls=%async_computation.1 | async-start | bytes 1310720 | tf_op jit(solution)/shard_map/psum | solution.py:50
Sparse Core Ops, SparseCore 0:
  65.1 110.4 all-reduce.5
  316.7 109.4 all-reduce.7
